TPU v7x, 32 devices: a whole 2x2x4 slice. The times are simulated.
32 devices in a mesh: cp: 16 (over z, x, core), tp: 2 (over y).
Axes of the slice: x: 2, y: 2, z: 4, core: 2. Of those that a mesh axis runs over, the one named last changes fastest.
Arguments:
- query: bfloat16 [1024, 16384], P(('cp', 'tp')), may hold values from -6 to 6
- fresh_key_rows: bfloat16 [1024, 1024], P(('cp', 'tp')), may hold values from -6 to 6
- fresh_value_rows: bfloat16 [1024, 1024], P(('cp', 'tp')), may hold values from -6 to 6
- cached_key_rows: bfloat16 [8192, 1024], P('cp', 'tp'), may hold values from -6 to 6
- cached_value_rows: bfloat16 [8192, 1024], P('cp', 'tp'), may hold values from -6 to 6
- prefix_len: int32 [1], replicated, may hold values from 4096 to 8192
- stripe_owner: int32 [16], replicated, may hold values from 0 to 15, each once
Outputs:
- attended: bfloat16 [1024, 16384], P('cp', 'tp')
Inputs may be any that keep to these rules, and one draw needn't show every extreme that they name: `stripe_owner`: a permutation of 0 to 15.
All inputs are finite; a program needn't handle non-finite values.
Results may differ from a plain program's by a relative error of at most 0.0075.
Values may be sent and summed in bfloat16 or wider, within the bound.
A program may use at most 64 MiB of HBM per device.

v0:
```python
import functools
import math

import jax
import jax.numpy as jnp
from jax import lax
from jax.experimental import pallas as pl
from jax.experimental.pallas import tpu as pltpu
from jax.sharding import PartitionSpec as P

HEAD_SIZE = 128
NEG = -1e30
EXPONENT = HEAD_SIZE ** (-0.5) * math.log2(math.e)


def attend_kernel(
    dims,
    plen_ref,
    q_ref,
    nat_ref,
    fresh_k,
    fresh_v,
    cache_k,
    cache_v,
    out_ref,
    m_ref,
    acc_ref,
    fresh_x,
    cache_x,
):
    per_step, chunk, fresh_chunk = dims
    rows = q_ref.shape[0]
    plen = plen_ref[0]

    @pl.when(pl.program_id(0) == 0)
    def _():
        for plain, wide in ((fresh_v, fresh_x), (cache_v, cache_x)):
            wide[:, :HEAD_SIZE] = plain[...]
            wide[:, HEAD_SIZE:] = jnp.ones(plain.shape, jnp.bfloat16)

    def piece(g, k, v, mask, first):
        q = q_ref[:, g * HEAD_SIZE : (g + 1) * HEAD_SIZE]
        s = lax.dot_general(q, k, (((1,), (1,)), ((), ())), preferred_element_type=jnp.float32)
        if mask is not None:
            s = jnp.where(mask, s, NEG)
        top = jnp.max(s, axis=1, keepdims=True)
        if first:
            m_new = jnp.broadcast_to(top, (rows, HEAD_SIZE))
        else:
            m_old = m_ref[g]
            m_new = jnp.maximum(m_old, top)
        p = jnp.exp2((s - m_new[:, :1]) * EXPONENT)
        o = jnp.dot(p.astype(jnp.bfloat16), v, preferred_element_type=jnp.float32)
        m_ref[g] = m_new
        if first:
            acc_ref[g] = o
        else:
            f = jnp.exp2((m_old - m_new) * EXPONENT)
            acc_ref[g, :, :HEAD_SIZE] = f * acc_ref[g, :, :HEAD_SIZE] + o[:, :HEAD_SIZE]
            acc_ref[g, :, HEAD_SIZE:] = f * acc_ref[g, :, HEAD_SIZE:] + o[:, HEAD_SIZE:]

    fresh = fresh_k.shape[0]
    for c in range(fresh // fresh_chunk):
        k = fresh_k[c * fresh_chunk : (c + 1) * fresh_chunk, :]
        v = fresh_x[c * fresh_chunk : (c + 1) * fresh_chunk, :]
        index = c * fresh_chunk + lax.broadcasted_iota(jnp.int32, (rows, fresh_chunk), 1)
        mask = index <= nat_ref[:, :1]
        for g in range(per_step):
            piece(g, k, v, mask, c == 0)

    def body(b, _):
        at = pl.multiple_of(b * chunk, chunk)
        k = cache_k[pl.ds(at, chunk), :]
        v = cache_x[pl.ds(at, chunk), :]
        for g in range(per_step):
            piece(g, k, v, None, False)
        return 0

    full = plen // chunk
    lax.fori_loop(0, full, body, 0)

    @pl.when(full * chunk < plen)
    def _():
        at = pl.multiple_of(full * chunk, chunk)
        k = cache_k[pl.ds(at, chunk), :]
        v = cache_x[pl.ds(at, chunk), :]
        index = at + lax.broadcasted_iota(jnp.int32, (1, chunk), 1)
        for g in range(per_step):
            piece(g, k, v, index < plen, False)

    for g in range(per_step):
        out_ref[:, g * HEAD_SIZE : (g + 1) * HEAD_SIZE] = (
            acc_ref[g, :, :HEAD_SIZE] / acc_ref[g, :, HEAD_SIZE:]
        ).astype(out_ref.dtype)


def attend(q, nat, fresh_k, fresh_v, cache_k, cache_v, prefix_len, per_step=4, chunk=1024):
    rows, columns = q.shape
    width = per_step * HEAD_SIZE
    fresh, slots = fresh_k.shape[0], cache_k.shape[0]
    whole = lambda i, *_: (0, 0)
    flops = 4 * rows * columns * (fresh + slots)
    return pl.pallas_call(
        functools.partial(attend_kernel, (per_step, min(chunk, slots), min(chunk, fresh))),
        out_shape=jax.ShapeDtypeStruct((rows, columns), jnp.bfloat16),
        grid_spec=pltpu.PrefetchScalarGridSpec(
            num_scalar_prefetch=1,
            grid=(columns // width,),
            in_specs=[
                pl.BlockSpec((rows, width), lambda i, *_: (0, i)),
                pl.BlockSpec((rows, HEAD_SIZE), whole),
                pl.BlockSpec((fresh, HEAD_SIZE), whole),
                pl.BlockSpec((fresh, HEAD_SIZE), whole),
                pl.BlockSpec((slots, HEAD_SIZE), whole),
                pl.BlockSpec((slots, HEAD_SIZE), whole),
            ],
            out_specs=pl.BlockSpec((rows, width), lambda i, *_: (0, i)),
            scratch_shapes=[
                pltpu.VMEM((per_step, rows, HEAD_SIZE), jnp.float32),
                pltpu.VMEM((per_step, rows, 2 * HEAD_SIZE), jnp.float32),
                pltpu.VMEM((fresh, 2 * HEAD_SIZE), jnp.bfloat16),
                pltpu.VMEM((slots, 2 * HEAD_SIZE), jnp.bfloat16),
            ],
        ),
        compiler_params=pltpu.CompilerParams(vmem_limit_bytes=56 * 1024 * 1024),
        cost_estimate=pl.CostEstimate(
            flops=flops, bytes_accessed=4 * fresh * columns, transcendentals=0
        ),
    )(prefix_len, q, nat, fresh_k, fresh_v, cache_k, cache_v)


def remote(source, target, send, receive, device):
    return pltpu.make_async_remote_copy(
        src_ref=source,
        dst_ref=target,
        send_sem=send,
        recv_sem=receive,
        device_id=device,
        device_id_type=pl.DeviceIdType.MESH,
    )


def greet(devices):
    barrier = pltpu.get_barrier_semaphore()
    for device in devices:
        pl.semaphore_signal(
            barrier, inc=1, device_id=device, device_id_type=pl.DeviceIdType.MESH
        )
    pl.semaphore_wait(barrier, len(devices))


def collect_kernel(
    heads,
    ranks,
    tps,
    cache_k,
    cache_v,
    fresh_k,
    fresh_v,
    all_ck,
    all_cv,
    all_fk,
    all_fv,
    local_k,
    local_v,
    tp_send,
    tp_recv,
    own_sem,
    z_send,
    z_recv,
    *rank_sems,
):
    me, tp = lax.axis_index("cp"), lax.axis_index("tp")
    row, rank = me // ranks, me % ranks
    arrays = ((cache_k, all_ck), (cache_v, all_cv), (local_k, all_fk), (local_v, all_fv))
    bits = []
    bit = ranks // 2
    while bit:
        bits.append(bit)
        bit //= 2
    partners = [rank + bit - 2 * bit * ((rank // bit) % 2) for bit in bits]
    column = [{"cp": (row + s) % heads * ranks + rank} for s in range(heads)]
    line = [{"cp": row * ranks + partner} for partner in partners]
    greet(column[1:] + line + [{"tp": (tp + t) % tps} for t in range(1, tps)])

    def cut(ref, head):
        return ref.at[:, pl.ds(pl.multiple_of(head * HEAD_SIZE, HEAD_SIZE), HEAD_SIZE)]

    def place(ref, index):
        block = ref.shape[0] // (heads * ranks)
        return ref.at[pl.ds(pl.multiple_of(index * block, block), block), :]

    started = []

    def go(copy):
        copy.start()
        started.append(copy)
        return copy

    def scatter(a):
        source, target = arrays[a]
        own = pltpu.make_async_copy(cut(source, row), place(target, me), own_sem.at[a])
        own.start()
        copies = [own]
        for s in range(1, heads):
            copies.append(
                go(
                    remote(
                        cut(source, (row + s) % heads),
                        place(target, me),
                        z_send.at[a, s],
                        z_recv.at[a, s],
                        column[s],
                    )
                )
            )
        return copies

    wide = heads * HEAD_SIZE
    few = fresh_k.shape[0]
    exchange = []
    for a, (source, target) in enumerate(((fresh_k, local_k), (fresh_v, local_v))):
        mine = target.at[pl.ds(pl.multiple_of(tp * few, few), few), :]
        for t in range(tps):
            to = (tp + t) % tps
            piece = source.at[:, pl.ds(pl.multiple_of(to * wide, wide), wide)]
            if t == 0:
                copy = pltpu.make_async_copy(piece, mine, own_sem.at[4 + a])
                copy.start()
            else:
                copy = go(remote(piece, mine, tp_send.at[a, t], tp_recv.at[a, t], {"tp": to}))
            exchange.append((t, copy))
    scattered = [scatter(0), scatter(1)]
    for t, copy in exchange:
        copy.wait() if t == 0 else copy.wait_recv()
    scattered += [scatter(2), scatter(3)]

    order = (0, 1, 2, 3)
    held = [(a, s, rank) for s in range(heads) for a in order]
    waits = {
        (a, s, 0): (scattered[a][s].wait if s == 0 else scattered[a][s].wait_recv)
        for a in order
        for s in range(heads)
    }
    held = [((a, s, 0), a, s, rank) for s in range(heads) for a in order]
    for level, partner in enumerate(partners):
        send, receive = rank_sems[2 * level], rank_sems[2 * level + 1]
        other = []
        for number, (key, a, s, owner) in enumerate(held):
            if waits.get(key) is not None:
                waits[key]()
                waits[key] = None
            index = (row + heads - s) % heads * ranks + owner
            target = arrays[a][1]
            copy = go(
                remote(
                    place(target, index),
                    place(target, index),
                    send.at[number],
                    receive.at[number],
                    line[level],
                )
            )
            bit = bits[level]
            name = (a, s, level + 1, number)
            waits[name] = copy.wait_recv
            other.append((name, a, s, owner + bit - 2 * bit * ((owner // bit) % 2)))
        held = held + other
    for wait in waits.values():
        if wait is not None:
            wait()
    for copy in started:
        copy.wait_send()


def collect_all(cache_k, cache_v, fresh_k, fresh_v, heads, ranks, tps):
    block, rows = cache_k.shape[0], fresh_k.shape[0] * tps
    wide = heads * HEAD_SIZE
    out = [
        jax.ShapeDtypeStruct((heads * ranks * n, HEAD_SIZE), jnp.bfloat16)
        for n in (block, block, rows, rows)
    ]
    rank_sems = []
    count = 4 * heads
    size = ranks
    while size > 1:
        rank_sems += [pltpu.SemaphoreType.DMA((count,))] * 2
        count *= 2
        size //= 2
    return pl.pallas_call(
        functools.partial(collect_kernel, heads, ranks, tps),
        out_shape=out,
        in_specs=[pl.BlockSpec(memory_space=pltpu.VMEM)] * 4,
        out_specs=[pl.BlockSpec(memory_space=pl.ANY)] * 4,
        scratch_shapes=[
            pltpu.VMEM((rows, wide), jnp.bfloat16),
            pltpu.VMEM((rows, wide), jnp.bfloat16),
            pltpu.SemaphoreType.DMA((2, tps)),
            pltpu.SemaphoreType.DMA((2, tps)),
            pltpu.SemaphoreType.DMA((6,)),
            pltpu.SemaphoreType.DMA((4, heads)),
            pltpu.SemaphoreType.DMA((4, heads)),
        ]
        + rank_sems,
        compiler_params=pltpu.CompilerParams(collective_id=1, has_side_effects=True),
        cost_estimate=pl.CostEstimate(flops=0, bytes_accessed=100000000, transcendentals=0),
    )(cache_k, cache_v, fresh_k, fresh_v)


def return_kernel(heads, ranks, done, out, own_sem, send, receive):
    me = lax.axis_index("cp")
    row, rank = me // ranks, me % ranks
    rows, width = out.shape[0], done.shape[1]
    column = [{"cp": (row + s) % heads * ranks + rank} for s in range(heads)]
    greet(column[1:])
    target = out.at[:, pl.ds(pl.multiple_of(row * width, width), width)]
    copies = []
    for s in list(range(1, heads)) + [0]:
        to = (row + s) % heads
        source = done.at[pl.ds(pl.multiple_of(to * rows, rows), rows), :]
        if s == 0:
            copy = pltpu.make_async_copy(source, target, own_sem)
        else:
            copy = remote(source, target, send.at[s], receive.at[s], column[s])
        copy.start()
        copies.append(copy)
    for copy in copies:
        copy.wait()


def give_back(done, heads, ranks):
    rows = done.shape[0] // heads
    return pl.pallas_call(
        functools.partial(return_kernel, heads, ranks),
        out_shape=jax.ShapeDtypeStruct((rows, heads * done.shape[1]), jnp.bfloat16),
        in_specs=[pl.BlockSpec(memory_space=pltpu.VMEM)],
        out_specs=pl.BlockSpec(memory_space=pltpu.VMEM),
        scratch_shapes=[
            pltpu.SemaphoreType.DMA,
            pltpu.SemaphoreType.DMA((heads,)),
            pltpu.SemaphoreType.DMA((heads,)),
        ],
        compiler_params=pltpu.CompilerParams(collective_id=2, has_side_effects=True),
        cost_estimate=pl.CostEstimate(flops=0, bytes_accessed=30000000, transcendentals=0),
    )(done)


def shards(
    query,
    fresh_key_rows,
    fresh_value_rows,
    cached_key_rows,
    cached_value_rows,
    prefix_len,
    stripe_owner,
):
    parts = lax.axis_size("cp")
    tps = lax.axis_size("tp")
    me = lax.axis_index("cp")
    heads = cached_key_rows.shape[1] // HEAD_SIZE
    ranks = parts // heads
    q_columns = query.shape[1] // tps // heads
    columns = [[h * ranks + r for h in range(heads)] for r in range(ranks)]
    lines = [[h * ranks + r for r in range(ranks)] for h in range(heads)]

    order = jnp.arange(parts, dtype=jnp.int32)
    inverse = jnp.sum(jnp.where(stripe_owner[None, :] == order[:, None], order[None, :], 0), axis=1)

    def split_heads(array):
        if heads == 1:
            return array
        return lax.all_to_all(
            array, "cp", split_axis=1, concat_axis=0, axis_index_groups=columns, tiled=True
        )

    def collect(array):
        block = array.shape[0]
        mine = split_heads(array)
        everything = lax.all_gather(mine, "cp", axis_index_groups=lines, tiled=True)
        return (
            everything.reshape(ranks, heads, block, HEAD_SIZE)
            .transpose(1, 0, 2, 3)
            .reshape(parts * block, HEAD_SIZE)
        )

    q_local = lax.all_to_all(query, "tp", split_axis=1, concat_axis=0, tiled=True)
    rows = q_local.shape[0]
    stripe = rows // parts

    by_rank = inverse.reshape(heads, ranks).T.reshape(-1)
    wanted = (by_rank[:, None] * stripe + jnp.arange(stripe, dtype=jnp.int32)[None, :]).reshape(-1)
    pick = (wanted[:, None] == jnp.arange(rows, dtype=jnp.int32)[None, :]).astype(jnp.bfloat16)
    q_sorted = jnp.dot(pick, q_local, preferred_element_type=jnp.float32).astype(jnp.bfloat16)
    q_out = (
        q_sorted.reshape(ranks, heads * stripe, heads, q_columns)
        .transpose(2, 0, 1, 3)
        .reshape(parts * heads * stripe, q_columns)
    )
    q_mine = lax.all_to_all(q_out, "cp", split_axis=0, concat_axis=0, tiled=True)

    if heads > 1 and ranks & (ranks - 1) == 0:
        cache_k, cache_v, fresh_k, fresh_v = collect_all(
            cached_key_rows, cached_value_rows, fresh_key_rows, fresh_value_rows, heads, ranks, tps
        )
    else:
        own = [
            lax.all_to_all(array, "tp", split_axis=1, concat_axis=0, tiled=True)
            for array in (fresh_key_rows, fresh_value_rows)
        ]
        cache_k, cache_v, fresh_k, fresh_v = (
            collect(array) for array in (cached_key_rows, cached_value_rows, *own)
        )

    rank = me % ranks
    residues = jnp.take(by_rank.reshape(ranks, heads), rank, axis=0)
    nat = (
        jnp.arange(parts, dtype=jnp.int32)[:, None, None] * rows
        + residues[None, :, None] * stripe
        + jnp.arange(stripe, dtype=jnp.int32)[None, None, :]
    ).reshape(-1, 1)
    nat = jnp.broadcast_to(nat, (nat.shape[0], HEAD_SIZE))

    done = attend(q_mine, nat, fresh_k, fresh_v, cache_k, cache_v, prefix_len)
    done = (
        done.reshape(parts, heads, stripe, q_columns)
        .transpose(1, 0, 2, 3)
        .reshape(heads * rows, q_columns)
    )
    if heads == 1:
        return done
    return give_back(done, heads, ranks)


def solution(mesh):
    return jax.shard_map(
        shards,
        mesh=mesh,
        in_specs=(
            P(("cp", "tp"), None),
            P(("cp", "tp"), None),
            P(("cp", "tp"), None),
            P("cp", "tp"),
            P("cp", "tp"),
            P(),
            P(),
        ),
        out_specs=P("cp", "tp"),
        check_vma=False,
    )
```

profile of v0, /device:TPU:0, one launch (start us, length us, event | category | flops | bytes accessed | tf_op | source)
XLA Modules:
  0.0 200.9 jit_solution(11814069723906786947)
XLA Ops:
  0.0 0.0 copy-start.1
  0.0 2.3 %copy.29 = bf16[4,2,8,8192]{3,2,0,1:T(8,128)(2,1)} copy(bf16[4,2,8,8192]{3,2,1,0:T(8,128)(2,1)} %bitcast.19) | data formatting | bytes 2097152 | tf_op jit(solution)/shard_map/all_to_all | solution.py:386
  2.3 4.3 %all-to-all-start = ((bf16[32,2,8192]{2,0,1:T(8,128)(2,1)}), bf16[32,2,8192]{2,0,1:T(8,128)(2,1)S(1)}, u32[]{:S(2)}, u32[]{:S(2)}) async-start(bf16[32,2,8192]{2,0,1:T(8,128)(2,1)} %bitcast.14), calls=%async_computation | async-start | bytes 2097152 | tf_op jit(solution)/shard_map/all_to_all | solution.py:386
  6.5 0.0 copy-done.1
  6.5 0.1 select_reduce_fusion
  6.7 0.1 reshape.101
  6.7 0.1 copy.22
  6.8 0.1 mul.28
  6.9 0.1 iota_add_fusion.1
  7.0 0.1 add.69
  7.1 13.9 %all-to-all-done = bf16[32,2,8192]{2,0,1:T(8,128)(2,1)S(1)} async-done(((bf16[32,2,8192]{2,0,1:T(8,128)(2,1)}), bf16[32,2,8192]{2,0,1:T(8,128)(2,1)S(1)}, u32[]{:S(2)}, u32[]{:S(2)}) %all-to-all-start) | async-done | bytes 1048608 | tf_op jit(solution)/shard_map/all_to_all | solution.py:386
  21.0 0.5 convolution_convert_fusion
  21.5 0.8 reshape.102
  22.3 1.5 copy.24
  23.8 6.1 %all-to-all-start.1 = ((bf16[16,16,2048]{2,1,0:T(8,128)(2,1)}), bf16[16,16,2048]{2,1,0:T(8,128)(2,1)S(1)}, u32[]{:S(2)}, u32[]{:S(2)}) async-start(bf16[16,16,2048]{2,1,0:T(8,128)(2,1)} %bitcast.4), calls=%async_computation.1 | async-start | bytes 2097152 | tf_op jit(solution)/shard_map/all_to_all | solution.py:399
  30.6 0.2 multiply_reduce_fusion
  30.8 0.1 broadcast_add_fusion
  30.9 0.1 iota_add_fusion
  31.0 0.1 add.78
  31.1 61.6 %shard_map.73 = (bf16[8192,128]{1,0:T(8,128)(2,1)}, bf16[8192,128]{1,0:T(8,128)(2,1)}, bf16[1024,128]{1,0:T(8,128)(2,1)}, bf16[1024,128]{1,0:T(8,128)(2,1)}) custom-call(bf16[512,512]{1,0:T(8,128)(2,1)} %cache_k.1, bf16[512,512]{1,0:T(8,128)(2,1)} %cache_v.1, bf16[32,1024]{1,0:T(8,128)(2,1)} %fresh_k.1, bf16[32,1024]{1,0:T(8,128)(2,1)} %fresh_v.1), custom_call_target="tpu_custom_call" | custom-call | bytes 100000000 | tf_op jit(solution)/shard_map/pallas_call | solution.py:290
  92.7 0.0 all-to-all-done.1
  92.7 0.0 copy-start
  92.7 0.8 broadcast_in_dim.37.nat_ref
  93.5 0.2 copy-done
  93.7 73.8 %shard_map.74 = bf16[256,2048]{1,0:T(8,128)(2,1)} custom-call(s32[1]{0:T(128)S(6)} %copy.32.plen_ref, bf16[256,2048]{1,0:T(8,128)(2,1)} %bitcast.20, s32[256,128]{1,0:T(8,128)} %broadcast_in_dim.37.nat_ref, bf16[1024,128]{1,0:T(8,128)(2,1)} %get-tuple-element.9.fresh_k, bf16[1024,128]{1,0:T(8,128)(2,1)} %get-tuple-element.10.fresh_v, ...), custom_call_target="tpu_custom_call" | custom-call | flops 19327352832 | bytes 8388608 | tf_op jit(solution)/shard_map/pallas_call | solution.py:103
  167.5 1.5 reshape.103
  169.0 0.6 copy.30
  169.6 1.1 reshape.104.done
  170.7 27.9 %shard_map.75 = bf16[64,8192]{1,0:T(8,128)(2,1)} custom-call(bf16[256,2048]{1,0:T(8,128)(2,1)} %reshape.104.done), custom_call_target="tpu_custom_call" | custom-call | bytes 30000000 | tf_op jit(solution)/shard_map/pallas_call | solution.py:333
  198.6 2.3 %copy.33 = bf16[64,8192]{1,0:T(8,128)(2,1)} copy(bf16[64,8192]{1,0:T(8,128)(2,1)} %shard_map.75) | data formatting | bytes 2097152
  (2 shorter events, 0.0 us)
Async XLA Ops:
  0.0 6.5 %copy-start.1 = (s32[16]{0:T(128)S(1)}, s32[16]{0:T(128)}, u32[]{:S(2)}) copy-start(s32[16]{0:T(128)} %param.13) | copy-start | bytes 196
  2.3 18.7 %all-to-all-start = ((bf16[32,2,8192]{2,0,1:T(8,128)(2,1)}), bf16[32,2,8192]{2,0,1:T(8,128)(2,1)S(1)}, u32[]{:S(2)}, u32[]{:S(2)}) async-start(bf16[32,2,8192]{2,0,1:T(8,128)(2,1)} %bitcast.14), calls=%async_computation | async-start | bytes 2097152 | tf_op jit(solution)/shard_map/all_to_all | solution.py:386
  23.8 68.9 %all-to-all-start.1 = ((bf16[16,16,2048]{2,1,0:T(8,128)(2,1)}), bf16[16,16,2048]{2,1,0:T(8,128)(2,1)S(1)}, u32[]{:S(2)}, u32[]{:S(2)}) async-start(bf16[16,16,2048]{2,1,0:T(8,128)(2,1)} %bitcast.4), calls=%async_computation.1 | async-start | bytes 2097152 | tf_op jit(solution)/shard_map/all_to_all | solution.py:399
  92.7 1.0 copy-start
where the time goes:
time: 200 us; the launch traced here: 201 us
  Pallas kernels  163 us (82%)
  waiting for transfers between devices  13.9 us (7%)
  local copies, waits for them, and re-layouts  11.5 us (6%)
  starting transfers between devices  10.4 us (5%)
    pallas_call x1, Pallas kernels, attend(): pl.pallas_call(functools.partial(attend_kernel, (per_step, min(chunk, slo...  73.8 us
    pallas_call x1, Pallas kernels, collect_all(): pl.pallas_call(functools.partial(collect_kernel, heads, ranks, tps), out_...  61.6 us
    pallas_call x1, Pallas kernels, give_back(): pl.pallas_call(functools.partial(return_kernel, heads, ranks), out_shape=...  27.9 us
    all_to_all x1, waiting for transfers between devices, shards(): lax.all_to_all(query, 'tp', split_axis=1, concat_axis=0, tiled=True)  13.9 us
    all_to_all x1, starting transfers between devices, shards(): lax.all_to_all(q_out, 'cp', split_axis=0, concat_axis=0, tiled=True)  6.13 us
    all_to_all x1, starting transfers between devices, shards(): lax.all_to_all(query, 'tp', split_axis=1, concat_axis=0, tiled=True)  4.26 us
  transfers between devices with their start and end apart: 2, of which 1 were waited for; matrix products, arithmetic and copies ran while one was open for 1% of the time, Pallas kernels for 31%

commit v1 on v0

v1 whole, which is shorter than its diff:
```python
import functools
import math

import jax
import jax.numpy as jnp
from jax import lax
from jax.experimental import pallas as pl
from jax.experimental.pallas import tpu as pltpu
from jax.sharding import PartitionSpec as P

HEAD_SIZE = 128
NEG = -1e30
EXPONENT = HEAD_SIZE ** (-0.5) * math.log2(math.e)


def attend_kernel(dims, plen_ref, q_ref, nat_ref, fresh_k, fresh_v, cache_k, cache_v, out_ref,
                  k2, vt, q2, s0, s1, m_ref, l_ref, acc_ref):
    per_step, chunk = dims
    rows = q_ref.shape[0]
    wide = rows * per_step
    plen = plen_ref[0]
    fresh, slots = fresh_k.shape[0], cache_k.shape[0]
    dn = (((1,), (1,)), ((), ()))

    @pl.when(pl.program_id(0) == 0)
    def _():
        eye = (lax.broadcasted_iota(jnp.int32, (HEAD_SIZE, HEAD_SIZE), 0)
               == lax.broadcasted_iota(jnp.int32, (HEAD_SIZE, HEAD_SIZE), 1)).astype(jnp.bfloat16)
        step = min(512, fresh)

        def prepare(source_k, source_v, base, count):
            def body(b, _):
                at = pl.multiple_of(b * step, step)
                to = pl.multiple_of(base + b * step, step)
                k = source_k[pl.ds(at, step), :]
                k2[pl.ds(to, step), :HEAD_SIZE] = k
                k2[pl.ds(to, step), HEAD_SIZE:] = k
                v = source_v[pl.ds(at, step), :]
                vt[:, pl.ds(to, step)] = lax.dot_general(
                    eye, v, dn, preferred_element_type=jnp.float32).astype(jnp.bfloat16)
                return 0
            lax.fori_loop(0, count // step, body, 0)
        prepare(fresh_k, fresh_v, 0, fresh)
        prepare(cache_k, cache_v, fresh, slots)

    for g in range(per_step):
        x = q_ref[:, g * HEAD_SIZE:(g + 1) * HEAD_SIZE].astype(jnp.float32) * EXPONENT
        x = x.T
        hi = x.astype(jnp.bfloat16)
        q2[:HEAD_SIZE, g * rows:(g + 1) * rows] = hi
        q2[HEAD_SIZE:, g * rows:(g + 1) * rows] = (x - hi.astype(jnp.float32)).astype(jnp.bfloat16)

    def score(at, s):
        s[...] = jnp.dot(k2[pl.ds(at, chunk), :], q2[...], preferred_element_type=jnp.float32)

    def soften(at, s_ref, mask, first):
        s = s_ref[...]
        if mask is not None:
            s = jnp.where(mask, s, NEG)
        top = jnp.max(s, axis=0, keepdims=True)
        m_new = top if first else jnp.maximum(m_ref[...], top)
        p = jnp.exp2(s - m_new)
        total = jnp.sum(p, axis=0, keepdims=True)
        o = jnp.dot(vt[:, pl.ds(at, chunk)], p.astype(jnp.bfloat16), preferred_element_type=jnp.float32)
        if first:
            l_ref[...] = total
            acc_ref[...] = o
        else:
            f = jnp.exp2(m_ref[...] - m_new)
            l_ref[...] = f * l_ref[...] + total
            acc_ref[...] = f * acc_ref[...] + o
        m_ref[...] = m_new

    bufs = (s0, s1)
    number = fresh // chunk
    assert number % 2 == 0
    nat = nat_ref[...]
    index = lax.broadcasted_iota(jnp.int32, (chunk, wide), 0)
    score(0, s0)
    for c in range(number):
        score((c + 1) * chunk, bufs[(c + 1) % 2])
        soften(c * chunk, bufs[c % 2], index + c * chunk <= nat, c == 0)

    pairs = (plen + 2 * chunk - 1) // (2 * chunk)

    def body(j, _):
        at = pl.multiple_of(fresh + 2 * j * chunk, chunk)
        score(pl.multiple_of(at + chunk, chunk), s1)
        soften(at, s0, None, False)
        score(pl.multiple_of(at + 2 * chunk, chunk), s0)
        soften(pl.multiple_of(at + chunk, chunk), s1, None, False)
        return 0
    lax.fori_loop(0, pairs - 1, body, 0)
    slot = 2 * (pairs - 1) * chunk
    at = pl.multiple_of(fresh + slot, chunk)
    score(pl.multiple_of(at + chunk, chunk), s1)
    soften(at, s0, index + slot < plen, False)
    soften(pl.multiple_of(at + chunk, chunk), s1, index + (slot + chunk) < plen, False)

    done = acc_ref[...] / l_ref[...]
    for g in range(per_step):
        out_ref[:, g * HEAD_SIZE:(g + 1) * HEAD_SIZE] = done[:, g * rows:(g + 1) * rows].T.astype(out_ref.dtype)


def attend(q, nat, fresh_k, fresh_v, cache_k, cache_v, prefix_len, chunk=512):
    rows, columns = q.shape
    per_step = nat.shape[1] // rows
    width = per_step * HEAD_SIZE
    wide = per_step * rows
    fresh, slots = fresh_k.shape[0], cache_k.shape[0]
    whole = lambda i, *_: (0, 0)
    keys = fresh + slots
    return pl.pallas_call(
        functools.partial(attend_kernel, (per_step, chunk)),
        out_shape=jax.ShapeDtypeStruct((rows, columns), jnp.bfloat16),
        grid_spec=pltpu.PrefetchScalarGridSpec(
            num_scalar_prefetch=1,
            grid=(columns // width,),
            in_specs=[
                pl.BlockSpec((rows, width), lambda i, *_: (0, i)),
                pl.BlockSpec((1, wide), whole),
                pl.BlockSpec((fresh, HEAD_SIZE), whole),
                pl.BlockSpec((fresh, HEAD_SIZE), whole),
                pl.BlockSpec((slots, HEAD_SIZE), whole),
                pl.BlockSpec((slots, HEAD_SIZE), whole),
            ],
            out_specs=pl.BlockSpec((rows, width), lambda i, *_: (0, i)),
            scratch_shapes=[
                pltpu.VMEM((keys, 2 * HEAD_SIZE), jnp.bfloat16),
                pltpu.VMEM((HEAD_SIZE, keys), jnp.bfloat16),
                pltpu.VMEM((2 * HEAD_SIZE, wide), jnp.bfloat16),
                pltpu.VMEM((chunk, wide), jnp.float32),
                pltpu.VMEM((chunk, wide), jnp.float32),
                pltpu.VMEM((1, wide), jnp.float32),
                pltpu.VMEM((1, wide), jnp.float32),
                pltpu.VMEM((HEAD_SIZE, wide), jnp.float32),
            ],
        ),
        compiler_params=pltpu.CompilerParams(vmem_limit_bytes=56 * 1024 * 1024),
        cost_estimate=pl.CostEstimate(flops=4*rows*columns*keys, bytes_accessed=4 * keys*HEAD_SIZE, transcendentals=0),
    )(prefix_len, q, nat, fresh_k, fresh_v, cache_k, cache_v)


def remote(source, target, send, receive, device):
    return pltpu.make_async_remote_copy(
        src_ref=source,
        dst_ref=target,
        send_sem=send,
        recv_sem=receive,
        device_id=device,
        device_id_type=pl.DeviceIdType.MESH,
    )


def greet(devices):
    barrier = pltpu.get_barrier_semaphore()
    for device in devices:
        pl.semaphore_signal(
            barrier, inc=1, device_id=device, device_id_type=pl.DeviceIdType.MESH
        )
    pl.semaphore_wait(barrier, len(devices))


def fused_kernel(
    sizes,
    plen_ref,
    nat_ref,
    pick_ref,
    query,
    fresh_k,
    fresh_v,
    cache_k,
    cache_v,
    out,
    k2,
    v_land,
    vt,
    q_land,
    o_buf,
    q2,
    s0,
    s1,
    m_ref,
    l_ref,
    acc_ref,
    fresh_send,
    fresh_recv,
    z_send,
    z_recv,
    q_send,
    q_recv,
    o_send,
    o_recv,
    *rank_sems,
):
    heads, ranks, tps, per_step, chunk = sizes
    parts = heads * ranks
    me, tp = lax.axis_index("cp"), lax.axis_index("tp")
    row, rank = me // ranks, me % ranks
    few = fresh_k.shape[0]
    block = cache_k.shape[0]
    fresh = parts * tps * few
    keys = k2.shape[0]
    slots = keys - fresh
    steps, rows, width = q_land.shape
    own_columns = steps * width
    wide = per_step * rows
    share = rows // parts
    dn = (((1,), (1,)), ((), ()))

    bits = []
    bit = ranks // 2
    while bit:
        bits.append(bit)
        bit //= 2
    partners = [rank + bit - 2 * bit * ((rank // bit) % 2) for bit in bits]
    line = [{"cp": row * ranks + partner} for partner in partners]

    def at_column(s, t):
        return {"cp": (row + s) % heads * ranks + rank, "tp": (tp + t) % tps}

    greet(
        [{"cp": (me + d) % parts} for d in range(1, parts)]
        + [at_column(s, t) for s in range(heads) for t in range(1, tps)]
    )

    def span(ref, start, size, step):
        return ref.at[pl.ds(pl.multiple_of(start, step), size), pl.ds(0, HEAD_SIZE)]

    def cut(ref, head):
        return ref.at[:, pl.ds(pl.multiple_of(head * HEAD_SIZE, HEAD_SIZE), HEAD_SIZE)]

    def place(a, index):
        target = k2 if a % 2 == 0 else v_land
        if a < 2:
            return span(target, fresh + index * block, block, block)
        return span(target, index * (tps * few), tps * few, tps * few)

    far = sorted(range(1, heads), key=lambda s: abs(2 * s - heads))
    shifts = [0] + far
    started = []

    def go(copy):
        copy.start()
        started.append(copy)
        return copy

    arrived = {}
    for s in shifts:
        for a, source in enumerate((cache_k, cache_v)):
            piece = cut(source, (row + s) % heads)
            if s == 0:
                copy = pltpu.make_async_copy(piece, place(a, me), z_recv.at[a, s])
                copy.start()
                arrived[a, s] = [copy.wait]
            else:
                copy = go(
                    remote(piece, place(a, me), z_send.at[a, s], z_recv.at[a, s], at_column(s, 0))
                )
                arrived[a, s] = [copy.wait_recv]
        for a, source in enumerate((fresh_k, fresh_v)):
            waits = []
            for t in range(tps):
                to = at_column(s, t)
                piece = cut(source, to["tp"] * heads + (row + s) % heads)
                target = span((k2, v_land)[a], me * (tps * few) + tp * few, few, few)
                if s == 0 and t == 0:
                    copy = pltpu.make_async_copy(piece, target, fresh_recv.at[a, s, t])
                    copy.start()
                    waits.append(copy.wait)
                else:
                    copy = go(
                        remote(
                            piece, target, fresh_send.at[a, s, t], fresh_recv.at[a, s, t], to
                        )
                    )
                    waits.append(copy.wait_recv)
            arrived[2 + a, s] = waits

    def query_copy(g, s, t, local):
        to = at_column(s, t)
        start = (to["tp"] * heads + (row + s) % heads) * own_columns + g * width
        source = query.at[:, pl.ds(pl.multiple_of(start, width), width)]
        target = q_land.at[g, pl.ds(pl.multiple_of((row * tps + tp) * few, few), few), :]
        if local:
            return pltpu.make_async_copy(source, target, q_recv.at[g, 0])
        return remote(source, target, q_send.at[g, s * tps + t], q_recv.at[g, s * tps + t], to)

    routes = [(s, t) for s in shifts for t in range(tps)]

    def send_query(g, _):
        for s, t in routes:
            query_copy(g, s, t, s == 0 and t == 0).start()
        return 0

    lax.fori_loop(0, steps, send_query, 0)

    order = (2, 3, 0, 1)
    held = [((a, s), a, s, rank) for s in shifts for a in order]
    for level, partner in enumerate(partners):
        send, receive = rank_sems[2 * level], rank_sems[2 * level + 1]
        other = []
        for number, (key, a, s, owner) in enumerate(held):
            for wait in arrived.pop(key, ()):
                wait()
            index = (row + heads - s) % heads * ranks + owner
            copy = go(
                remote(
                    place(a, index), place(a, index), send.at[number], receive.at[number], line[level]
                )
            )
            bit = bits[level]
            name = (a, s, level + 1, number)
            arrived[name] = [copy.wait_recv]
            other.append((name, a, s, owner + bit - 2 * bit * ((owner // bit) % 2)))
        held = held + other
    for waits in arrived.values():
        for wait in waits:
            wait()

    eye = (
        lax.broadcasted_iota(jnp.int32, (HEAD_SIZE, HEAD_SIZE), 0)
        == lax.broadcasted_iota(jnp.int32, (HEAD_SIZE, HEAD_SIZE), 1)
    ).astype(jnp.bfloat16)

    def prepare(b, _):
        at = pl.multiple_of(b * chunk, chunk)
        k2[pl.ds(at, chunk), HEAD_SIZE:] = k2[pl.ds(at, chunk), :HEAD_SIZE]
        vt[:, pl.ds(at, chunk)] = lax.dot_general(
            eye, v_land[pl.ds(at, chunk), :], dn, preferred_element_type=jnp.float32
        ).astype(jnp.bfloat16)
        return 0

    lax.fori_loop(0, keys // chunk, prepare, 0)

    def score(at, s):
        s[...] = jnp.dot(k2[pl.ds(at, chunk), :], q2[...], preferred_element_type=jnp.float32)

    def soften(at, s_ref, mask, first):
        s = s_ref[...]
        if mask is not None:
            s = jnp.where(mask, s, NEG)
        top = jnp.max(s, axis=0, keepdims=True)
        m_new = top if first else jnp.maximum(m_ref[...], top)
        p = jnp.exp2(s - m_new)
        total = jnp.sum(p, axis=0, keepdims=True)
        o = jnp.dot(
            vt[:, pl.ds(at, chunk)], p.astype(jnp.bfloat16), preferred_element_type=jnp.float32
        )
        if first:
            l_ref[...] = total
            acc_ref[...] = o
        else:
            f = jnp.exp2(m_ref[...] - m_new)
            l_ref[...] = f * l_ref[...] + total
            acc_ref[...] = f * acc_ref[...] + o
        m_ref[...] = m_new

    def output_copy(g, d):
        to = (me + d) % parts
        columns = pl.ds(pl.multiple_of(g * width, width), width)
        source = o_buf.at[pl.ds(pl.multiple_of(to * share, share), share), columns]
        target = out.at[
            pl.ds(pl.multiple_of(rank * share, share), share),
            pl.ds(pl.multiple_of(row * own_columns + g * width, width), width),
        ]
        if d == 0:
            return pltpu.make_async_copy(source, target, o_recv.at[g, 0])
        return remote(source, target, o_send.at[g, d], o_recv.at[g, d], {"cp": to})

    def send_output(g):
        for d in range(parts):
            output_copy(g, d).start()

    bufs = (s0, s1)
    number = fresh // chunk
    index = lax.broadcasted_iota(jnp.int32, (chunk, wide), 0)
    pairs = slots // (2 * chunk)
    sure = pairs // 2

    def step(g, _):
        for s, t in routes:
            if s == 0 and t == 0:
                query_copy(g, s, t, True).wait()
            else:
                query_copy(g, s, t, False).wait_recv()
        pick = pick_ref[...]
        for h in range(per_step):
            x = jnp.dot(
                pick,
                q_land[g, :, h * HEAD_SIZE : (h + 1) * HEAD_SIZE],
                preferred_element_type=jnp.float32,
            )
            x = x.T * EXPONENT
            hi = x.astype(jnp.bfloat16)
            q2[:HEAD_SIZE, h * rows : (h + 1) * rows] = hi
            q2[HEAD_SIZE:, h * rows : (h + 1) * rows] = (x - hi.astype(jnp.float32)).astype(
                jnp.bfloat16
            )

        @pl.when(g > 0)
        def _():
            send_output(g - 1)

        nat = nat_ref[...]
        score(0, s0)
        for c in range(number):
            score((c + 1) * chunk, bufs[(c + 1) % 2])
            soften(c * chunk, bufs[c % 2], index + c * chunk <= nat, c == 0)

        def pair(masked, last, j):
            slot = 2 * j * chunk
            at = pl.multiple_of(fresh + slot, chunk)
            score(pl.multiple_of(at + chunk, chunk), s1)
            soften(at, s0, index + slot < plen_ref[...] if masked else None, False)
            if not last:
                score(pl.multiple_of(at + 2 * chunk, chunk), s0)
            soften(
                pl.multiple_of(at + chunk, chunk),
                s1,
                index + (slot + chunk) < plen_ref[...] if masked else None,
                False,
            )

        def plain(j, _):
            pair(False, False, j)
            return 0

        def masked(j, _):
            pair(True, False, j)
            return 0

        lax.fori_loop(0, sure, plain, 0)
        lax.fori_loop(sure, pairs - 1, masked, 0)
        pair(True, True, pairs - 1)

        done = acc_ref[...] / l_ref[...]
        for h in range(per_step):
            columns = pl.ds(pl.multiple_of(g * width + h * HEAD_SIZE, HEAD_SIZE), HEAD_SIZE)
            o_buf[:, columns] = done[:, h * rows : (h + 1) * rows].T.astype(o_buf.dtype)
        return 0

    lax.fori_loop(0, steps, step, 0)
    send_output(steps - 1)

    def finish(g, _):
        for s, t in routes:
            if s != 0 or t != 0:
                query_copy(g, s, t, False).wait_send()
        for d in range(parts):
            output_copy(g, d).wait()
        return 0

    for copy in started:
        copy.wait_send()
    lax.fori_loop(0, steps, finish, 0)


def fused(
    plen, nat, pick, query, fresh_k, fresh_v, cache_k, cache_v, heads, ranks, tps, per_step, chunk
):
    parts = heads * ranks
    few, block = fresh_k.shape[0], cache_k.shape[0]
    fresh = parts * tps * few
    keys = fresh + parts * block
    rows = heads * tps * few
    width = per_step * HEAD_SIZE
    wide = per_step * rows
    own_columns = query.shape[1] // (tps * heads)
    steps = own_columns // width
    rank_sems = []
    count = 4 * heads
    size = ranks
    while size > 1:
        rank_sems += [pltpu.SemaphoreType.DMA((count,))] * 2
        count *= 2
        size //= 2
    dma = pltpu.SemaphoreType.DMA
    b16, f32 = jnp.bfloat16, jnp.float32
    return pl.pallas_call(
        functools.partial(fused_kernel, (heads, ranks, tps, per_step, chunk)),
        out_shape=jax.ShapeDtypeStruct((tps * few, heads * own_columns), b16),
        in_specs=[pl.BlockSpec(memory_space=pltpu.VMEM)] * 3
        + [pl.BlockSpec(memory_space=pl.ANY)] * 5,
        out_specs=pl.BlockSpec(memory_space=pl.ANY),
        scratch_shapes=[
            pltpu.VMEM((keys, 2 * HEAD_SIZE), b16),
            pltpu.VMEM((keys, HEAD_SIZE), b16),
            pltpu.VMEM((HEAD_SIZE, keys), b16),
            pltpu.VMEM((steps, rows, width), b16),
            pltpu.VMEM((rows, own_columns), b16),
            pltpu.VMEM((2 * HEAD_SIZE, wide), b16),
            pltpu.VMEM((chunk, wide), f32),
            pltpu.VMEM((chunk, wide), f32),
            pltpu.VMEM((1, wide), f32),
            pltpu.VMEM((1, wide), f32),
            pltpu.VMEM((HEAD_SIZE, wide), f32),
            dma((2, heads, tps)),
            dma((2, heads, tps)),
            dma((2, heads)),
            dma((2, heads)),
            dma((steps, heads * tps)),
            dma((steps, heads * tps)),
            dma((steps, parts)),
            dma((steps, parts)),
        ]
        + rank_sems,
        compiler_params=pltpu.CompilerParams(
            collective_id=1, has_side_effects=True, vmem_limit_bytes=56 * 1024 * 1024
        ),
        cost_estimate=pl.CostEstimate(
            flops=4 * rows * own_columns * keys, bytes_accessed=100000000, transcendentals=0
        ),
    )(plen, nat, pick, query, fresh_k, fresh_v, cache_k, cache_v)


def exchanged(
    query, fresh_key_rows, fresh_value_rows, cached_key_rows, cached_value_rows, prefix_len, inverse
):
    parts, tps = lax.axis_size("cp"), lax.axis_size("tp")
    heads = cached_key_rows.shape[1] // HEAD_SIZE
    ranks = parts // heads
    rank = lax.axis_index("cp") % ranks
    few = fresh_key_rows.shape[0]
    many = tps * few
    stripe = many // parts
    rows = heads * many
    group = query.shape[1] // (tps * heads * HEAD_SIZE)
    per_step = max(1, min(group, 512 // rows))
    fresh = parts * many
    chunk = min(512, fresh // 2)
    z = jnp.arange(heads, dtype=jnp.int32)[None, :, None]
    i = jnp.arange(stripe, dtype=jnp.int32)[None, None, :]
    inside = inverse[:, None, None] * stripe + i
    local = (z * many + inside).reshape(rows)
    nat = ((z * ranks + rank) * many + inside).reshape(rows)
    nat = jnp.tile(nat[None, :], (1, per_step))
    pick = (local[:, None] == jnp.arange(rows, dtype=jnp.int32)[None, :]).astype(jnp.bfloat16)
    plen = jnp.broadcast_to(prefix_len[None, :], nat.shape)
    landed = fused(
        plen,
        nat,
        pick,
        query,
        fresh_key_rows,
        fresh_value_rows,
        cached_key_rows,
        cached_value_rows,
        heads,
        ranks,
        tps,
        per_step,
        chunk,
    )
    return (
        landed.reshape(ranks, heads, stripe, landed.shape[1])
        .transpose(1, 0, 2, 3)
        .reshape(landed.shape)
    )


def plain(
    query, fresh_key_rows, fresh_value_rows, cached_key_rows, cached_value_rows, prefix_len, inverse
):
    parts = lax.axis_size("cp")
    me = lax.axis_index("cp")
    heads = cached_key_rows.shape[1] // HEAD_SIZE
    ranks = parts // heads
    tps = lax.axis_size("tp")
    q_columns = query.shape[1] // tps // heads
    columns = [[h * ranks + r for h in range(heads)] for r in range(ranks)]
    lines = [[h * ranks + r for r in range(ranks)] for h in range(heads)]

    def split_heads(array, axis_name="cp"):
        if heads == 1:
            return array
        return lax.all_to_all(
            array, axis_name, split_axis=1, concat_axis=0, axis_index_groups=columns, tiled=True
        )

    def collect(array):
        block = array.shape[0]
        mine = split_heads(array)
        everything = lax.all_gather(mine, "cp", axis_index_groups=lines, tiled=True)
        return (
            everything.reshape(ranks, heads, block, HEAD_SIZE)
            .transpose(1, 0, 2, 3)
            .reshape(parts * block, HEAD_SIZE)
        )

    q_local = lax.all_to_all(query, "tp", split_axis=1, concat_axis=0, tiled=True)
    rows = q_local.shape[0]
    stripe = rows // parts
    by_rank = inverse.reshape(heads, ranks).T.reshape(-1)
    wanted = (by_rank[:, None] * stripe + jnp.arange(stripe, dtype=jnp.int32)[None, :]).reshape(-1)
    pick = (wanted[:, None] == jnp.arange(rows, dtype=jnp.int32)[None, :]).astype(jnp.bfloat16)
    q_sorted = jnp.dot(pick, q_local, preferred_element_type=jnp.float32).astype(jnp.bfloat16)
    q_out = (
        q_sorted.reshape(ranks, heads * stripe, heads, q_columns)
        .transpose(2, 0, 1, 3)
        .reshape(parts * heads * stripe, q_columns)
    )
    q_mine = lax.all_to_all(q_out, "cp", split_axis=0, concat_axis=0, tiled=True)
    own = [
        lax.all_to_all(array, "tp", split_axis=1, concat_axis=0, tiled=True)
        for array in (fresh_key_rows, fresh_value_rows)
    ]
    cache_k, cache_v, fresh_k, fresh_v = (
        collect(array) for array in (cached_key_rows, cached_value_rows, *own)
    )
    residues = jnp.take(by_rank.reshape(ranks, heads), me % ranks, axis=0)
    nat = (
        jnp.arange(parts, dtype=jnp.int32)[:, None, None] * rows
        + residues[None, :, None] * stripe
        + jnp.arange(stripe, dtype=jnp.int32)[None, None, :]
    ).reshape(1, -1)
    per_step = max(1, min(q_columns // HEAD_SIZE, 512 // nat.shape[1]))
    nat = jnp.tile(nat, (1, per_step))
    done = attend(q_mine, nat, fresh_k, fresh_v, cache_k, cache_v, prefix_len)
    done = (
        done.reshape(parts, heads, stripe, q_columns)
        .transpose(1, 0, 2, 3)
        .reshape(heads * rows, q_columns)
    )
    if heads == 1:
        return done
    split = done.reshape(heads, rows, q_columns)
    back = lax.all_to_all(
        split, "cp", split_axis=0, concat_axis=0, axis_index_groups=columns, tiled=True
    )
    return back.transpose(1, 0, 2).reshape(rows, heads * q_columns)


def shards(
    query,
    fresh_key_rows,
    fresh_value_rows,
    cached_key_rows,
    cached_value_rows,
    prefix_len,
    stripe_owner,
):
    parts = lax.axis_size("cp")
    heads = cached_key_rows.shape[1] // HEAD_SIZE
    ranks = parts // heads
    order = jnp.arange(parts, dtype=jnp.int32)
    inverse = jnp.sum(jnp.where(stripe_owner[None, :] == order[:, None], order[None, :], 0), axis=1)
    path = exchanged if heads > 1 and ranks & (ranks - 1) == 0 else plain
    return path(
        query,
        fresh_key_rows,
        fresh_value_rows,
        cached_key_rows,
        cached_value_rows,
        prefix_len,
        inverse,
    )


def solution(mesh):
    return jax.shard_map(
        shards,
        mesh=mesh,
        in_specs=(
            P(("cp", "tp"), None),
            P(("cp", "tp"), None),
            P(("cp", "tp"), None),
            P("cp", "tp"),
            P("cp", "tp"),
            P(),
            P(),
        ),
        out_specs=P("cp", "tp"),
        check_vma=False,
    )
```

time: 200 us -> 141 us (0.70)
  Pallas kernels: 163 us -> 134 us
  waiting for transfers between devices: 13.9 us -> 0 us
  starting transfers between devices: 10.4 us -> 0 us
  local copies, waits for them, and re-layouts: 11.5 us -> 4.99 us
    pallas_call x3 -> x1, Pallas kernels: 163 us -> 134 us  [fused(): pl.pallas_call(functools.partial(fused_kernel, (heads, ranks, tps, per_st...]
    all_to_all x2 -> x0, waiting for transfers between devices: 13.9 us -> none  [the longest x1 13.9 us: shards(): lax.all_to_all(query, 'tp', split_axis=1, concat_axis=0, tiled=True)]
    all_to_all x2 -> x0, starting transfers between devices: 10.4 us -> none  [the longest x1 6.13 us: shards(): lax.all_to_all(q_out, 'cp', split_axis=0, concat_axis=0, tiled=True)]
    all_to_all x1 -> x0, local copies, waits for them, and re-layouts: 2.27 us -> none  [shards(): lax.all_to_all(query, 'tp', split_axis=1, concat_axis=0, tiled=True)]
    reshape x5 -> x2, local copies, waits for them, and re-layouts: 4.01 us -> 2.56 us  [the longest x1 1.46 us: exchanged(): landed.reshape(ranks, heads, stripe, landed.shape[1]).transpose(1, 0, 2, 3)]
  transfers between devices with their start and end apart: 2 -> 0, of which waited for: 1 -> 0; matrix products, arithmetic and copies ran while one was open for 1% -> 0% of each run, Pallas kernels for 31% -> 0%
where the time goes in v1:
time: 141 us
  Pallas kernels  134 us (95%)
  local copies, waits for them, and re-layouts  4.99 us (4%)
    pallas_call x1, Pallas kernels, fused(): pl.pallas_call(functools.partial(fused_kernel, (heads, ranks, tps, per_st...  134 us

profile of v1, /device:TPU:0, one launch (start us, length us, event | category | flops | bytes accessed | tf_op | source)
XLA Modules:
  0.0 141.0 jit_solution(11691027951320546139)
XLA Ops:
  0.7 0.0 copy-start
  0.7 0.6 copy-done
  1.3 0.1 select_reduce_fusion
  1.4 0.6 broadcast_in_dim.17.plen_ref
  2.0 0.1 iota_add_fusion
  2.1 0.1 broadcast_add_fusion
  2.2 0.1 add.83
  2.3 0.1 add.80
  2.4 0.6 copy.11
  3.0 0.8 fusion.pick_ref
  3.8 134.3 %shard_map.73 = bf16[64,8192]{1,0:T(8,128)(2,1)} custom-call(s32[1,512]{1,0:T(1,128)} %broadcast_in_dim.17.plen_ref, s32[1,512]{1,0:T(1,128)} %bitcast.8, bf16[256,256]{1,0:T(8,128)(2,1)} %fusion.pick_ref, bf16[32,16384]{1,0:T(8,128)(2,1)} %query.1, bf16[32,1024]{1,0:T(8,128)(2,1)} %fresh_k.1, bf16[32,1024]{1,0:T(8,128)(2,1)} %fresh_v.1, ...), custom_call_target="tpu_custom_call" | custom-call | flops 19327352832 | bytes 100000000 | tf_op jit(solution)/shard_map/pallas_call | solution.py:480
  138.1 1.5 %reshape.83 = bf16[4,4,4,8192]{3,2,1,0:T(4,128)(2,1)S(1)} reshape(bf16[64,8192]{1,0:T(8,128)(2,1)} %shard_map.73) | data formatting | bytes 2097152 | tf_op jit(solution)/shard_map/reshape | solution.py:556
  139.5 0.4 copy.10
  139.9 1.1 reshape.84
  (3 shorter events, 0.0 us)
Async XLA Ops:
  0.7 0.7 copy-start

commit v2 on v1

--- a/solution.py
+++ b/solution.py
@@ -164,8 +164,7 @@
 def fused_kernel(
     sizes,
     plen_ref,
-    nat_ref,
-    pick_ref,
+    owner_ref,
     query,
     fresh_k,
     fresh_v,
@@ -178,8 +177,11 @@
     q_land,
     o_buf,
     q2,
+    pick_ref,
     s0,
     s1,
+    t0,
+    t1,
     m_ref,
     l_ref,
     acc_ref,
@@ -191,6 +193,7 @@
     q_recv,
     o_send,
     o_recv,
+    twin_sem,
     *rank_sems,
 ):
     heads, ranks, tps, per_step, chunk = sizes
@@ -216,8 +219,17 @@
     partners = [rank + bit - 2 * bit * ((rank // bit) % 2) for bit in bits]
     line = [{"cp": row * ranks + partner} for partner in partners]
 
+    def peer(s):
+        other = row
+        bit = 1
+        while bit <= s:
+            if s & bit:
+                other = other + bit - 2 * bit * ((other // bit) % 2)
+            bit *= 2
+        return other
+
     def at_column(s, t):
-        return {"cp": (row + s) % heads * ranks + rank, "tp": (tp + t) % tps}
+        return {"cp": peer(s) * ranks + rank, "tp": (tp + t) % tps}
 
     greet(
         [{"cp": (me + d) % parts} for d in range(1, parts)]
@@ -236,8 +248,7 @@
             return span(target, fresh + index * block, block, block)
         return span(target, index * (tps * few), tps * few, tps * few)
 
-    far = sorted(range(1, heads), key=lambda s: abs(2 * s - heads))
-    shifts = [0] + far
+    shifts = range(heads)
     started = []
 
     def go(copy):
@@ -248,7 +259,7 @@
     arrived = {}
     for s in shifts:
         for a, source in enumerate((cache_k, cache_v)):
-            piece = cut(source, (row + s) % heads)
+            piece = cut(source, peer(s))
             if s == 0:
                 copy = pltpu.make_async_copy(piece, place(a, me), z_recv.at[a, s])
                 copy.start()
@@ -262,7 +273,7 @@
             waits = []
             for t in range(tps):
                 to = at_column(s, t)
-                piece = cut(source, to["tp"] * heads + (row + s) % heads)
+                piece = cut(source, to["tp"] * heads + peer(s))
                 target = span((k2, v_land)[a], me * (tps * few) + tp * few, few, few)
                 if s == 0 and t == 0:
                     copy = pltpu.make_async_copy(piece, target, fresh_recv.at[a, s, t])
@@ -279,7 +290,7 @@
 
     def query_copy(g, s, t, local):
         to = at_column(s, t)
-        start = (to["tp"] * heads + (row + s) % heads) * own_columns + g * width
+        start = (to["tp"] * heads + peer(s)) * own_columns + g * width
         source = query.at[:, pl.ds(pl.multiple_of(start, width), width)]
         target = q_land.at[g, pl.ds(pl.multiple_of((row * tps + tp) * few, few), few), :]
         if local:
@@ -303,7 +314,7 @@
         for number, (key, a, s, owner) in enumerate(held):
             for wait in arrived.pop(key, ()):
                 wait()
-            index = (row + heads - s) % heads * ranks + owner
+            index = peer(s) * ranks + owner
             copy = go(
                 remote(
                     place(a, index), place(a, index), send.at[number], receive.at[number], line[level]
@@ -314,9 +325,39 @@
             arrived[name] = [copy.wait_recv]
             other.append((name, a, s, owner + bit - 2 * bit * ((owner // bit) % 2)))
         held = held + other
-    for waits in arrived.values():
-        for wait in waits:
+    twins = []
+
+    def twin(number, start, size):
+        copy = pltpu.make_async_copy(
+            span(k2, start, size, size),
+            k2.at[pl.ds(pl.multiple_of(start, size), size), pl.ds(HEAD_SIZE, HEAD_SIZE)],
+            twin_sem.at[number],
+        )
+        copy.start()
+        twins.append(copy)
+
+    lane = lax.broadcasted_iota(jnp.int32, (rows, rows), 1)
+    sorted_row = lax.broadcasted_iota(jnp.int32, (rows, rows), 0)
+
+    def natural(at):
+        many = tps * few
+        stripe = many // parts
+        inside = jnp.zeros(at.shape, jnp.int32)
+        for r in range(parts):
+            inside = jnp.where(at // share == owner_ref[r], r * stripe, inside)
+        return at % share // stripe, inside + at % stripe
+
+    z, inside = natural(sorted_row)
+    pick_ref[...] = (z * (tps * few) + inside == lane).astype(jnp.float32).astype(jnp.bfloat16)
+
+    for key, a, s, owner in held:
+        for wait in arrived.pop(key, ()):
             wait()
+        index = peer(s) * ranks + owner
+        if a == 0:
+            twin(len(twins), fresh + index * block, block)
+        elif a == 2:
+            twin(len(twins), index * (tps * few), tps * few)
 
     eye = (
         lax.broadcasted_iota(jnp.int32, (HEAD_SIZE, HEAD_SIZE), 0)
@@ -325,36 +366,46 @@
 
     def prepare(b, _):
         at = pl.multiple_of(b * chunk, chunk)
-        k2[pl.ds(at, chunk), HEAD_SIZE:] = k2[pl.ds(at, chunk), :HEAD_SIZE]
         vt[:, pl.ds(at, chunk)] = lax.dot_general(
             eye, v_land[pl.ds(at, chunk), :], dn, preferred_element_type=jnp.float32
         ).astype(jnp.bfloat16)
         return 0
 
     lax.fori_loop(0, keys // chunk, prepare, 0)
-
-    def score(at, s):
-        s[...] = jnp.dot(k2[pl.ds(at, chunk), :], q2[...], preferred_element_type=jnp.float32)
-
-    def soften(at, s_ref, mask, first):
-        s = s_ref[...]
+    for copy in twins:
+        copy.wait()
+
+    slabs = ((s0, t0), (s1, t1))
+
+    def score(at, slab, h, mask):
+        s_ref, t_ref = slabs[slab]
+        s = jnp.dot(
+            k2[pl.ds(at, chunk), :],
+            q2[:, h * rows : (h + 1) * rows],
+            preferred_element_type=jnp.float32,
+        )
         if mask is not None:
             s = jnp.where(mask, s, NEG)
-        top = jnp.max(s, axis=0, keepdims=True)
-        m_new = top if first else jnp.maximum(m_ref[...], top)
-        p = jnp.exp2(s - m_new)
+        s_ref[h] = s
+        t_ref[h] = jnp.max(s, axis=0, keepdims=True)
+
+    def soften(at, slab, h, first):
+        s_ref, t_ref = slabs[slab]
+        top = t_ref[h]
+        m_new = top if first else jnp.maximum(m_ref[h], top)
+        p = jnp.exp2(s_ref[h] - m_new)
         total = jnp.sum(p, axis=0, keepdims=True)
         o = jnp.dot(
             vt[:, pl.ds(at, chunk)], p.astype(jnp.bfloat16), preferred_element_type=jnp.float32
         )
         if first:
-            l_ref[...] = total
-            acc_ref[...] = o
+            l_ref[h] = total
+            acc_ref[h] = o
         else:
-            f = jnp.exp2(m_ref[...] - m_new)
-            l_ref[...] = f * l_ref[...] + total
-            acc_ref[...] = f * acc_ref[...] + o
-        m_ref[...] = m_new
+            f = jnp.exp2(m_ref[h] - m_new)
+            l_ref[h] = f * l_ref[h] + total
+            acc_ref[h] = f * acc_ref[h] + o
+        m_ref[h] = m_new
 
     def output_copy(g, d):
         to = (me + d) % parts
@@ -372,11 +423,11 @@
         for d in range(parts):
             output_copy(g, d).start()
 
-    bufs = (s0, s1)
     number = fresh // chunk
-    index = lax.broadcasted_iota(jnp.int32, (chunk, wide), 0)
-    pairs = slots // (2 * chunk)
-    sure = pairs // 2
+    units = slots // chunk
+    group = 4
+    index = lax.broadcasted_iota(jnp.int32, (chunk, rows), 0)
+    sure = (units // 2 - 1) // group
 
     def step(g, _):
         for s, t in routes:
@@ -384,10 +435,9 @@
                 query_copy(g, s, t, True).wait()
             else:
                 query_copy(g, s, t, False).wait_recv()
-        pick = pick_ref[...]
         for h in range(per_step):
             x = jnp.dot(
-                pick,
+                pick_ref[...],
                 q_land[g, :, h * HEAD_SIZE : (h + 1) * HEAD_SIZE],
                 preferred_element_type=jnp.float32,
             )
@@ -402,42 +452,45 @@
         def _():
             send_output(g - 1)
 
-        nat = nat_ref[...]
-        score(0, s0)
+        z, inside = natural(lax.broadcasted_iota(jnp.int32, (1, rows), 1))
+        nat = (z * ranks + rank) * (tps * few) + inside
+        for h in range(per_step):
+            score(0, 0, h, index <= nat)
         for c in range(number):
-            score((c + 1) * chunk, bufs[(c + 1) % 2])
-            soften(c * chunk, bufs[c % 2], index + c * chunk <= nat, c == 0)
-
-        def pair(masked, last, j):
-            slot = 2 * j * chunk
-            at = pl.multiple_of(fresh + slot, chunk)
-            score(pl.multiple_of(at + chunk, chunk), s1)
-            soften(at, s0, index + slot < plen_ref[...] if masked else None, False)
-            if not last:
-                score(pl.multiple_of(at + 2 * chunk, chunk), s0)
-            soften(
-                pl.multiple_of(at + chunk, chunk),
-                s1,
-                index + (slot + chunk) < plen_ref[...] if masked else None,
-                False,
-            )
-
-        def plain(j, _):
-            pair(False, False, j)
+            for h in range(per_step):
+                if c + 1 < number:
+                    score((c + 1) * chunk, (c + 1) % 2, h, index + (c + 1) * chunk <= nat)
+                else:
+                    score(fresh, 0, h, None)
+                soften(c * chunk, c % 2, h, c == 0)
+
+        def batch(masked, j):
+            for u in range(group):
+                slot = (j * group + u) * chunk
+                after = slot + chunk
+                mask = index + after < plen_ref[0] if masked else None
+                for h in range(per_step):
+                    score(pl.multiple_of(fresh + after, chunk), (u + 1) % 2, h, mask)
+                    soften(pl.multiple_of(fresh + slot, chunk), u % 2, h, False)
             return 0
 
-        def masked(j, _):
-            pair(True, False, j)
-            return 0
-
-        lax.fori_loop(0, sure, plain, 0)
-        lax.fori_loop(sure, pairs - 1, masked, 0)
-        pair(True, True, pairs - 1)
-
-        done = acc_ref[...] / l_ref[...]
-        for h in range(per_step):
+        def finish_head(h):
             columns = pl.ds(pl.multiple_of(g * width + h * HEAD_SIZE, HEAD_SIZE), HEAD_SIZE)
-            o_buf[:, columns] = done[:, h * rows : (h + 1) * rows].T.astype(o_buf.dtype)
+            o_buf[:, columns] = (acc_ref[h] / l_ref[h]).T.astype(o_buf.dtype)
+
+        if sure == 1:
+            batch(False, 0)
+        else:
+            lax.fori_loop(0, sure, lambda j, _: batch(False, j), 0)
+        lax.fori_loop(sure, units // group - 1, lambda j, _: batch(True, j), 0)
+        for u in range(units - group, units):
+            for h in range(per_step):
+                if u + 1 < units:
+                    after = (u + 1) * chunk
+                    score(fresh + after, (u + 1) % 2, h, index + after < plen_ref[0])
+                soften(fresh + u * chunk, u % 2, h, False)
+                if u + 1 == units:
+                    finish_head(h)
         return 0
 
     lax.fori_loop(0, steps, step, 0)
@@ -457,7 +510,7 @@
 
 
 def fused(
-    plen, nat, pick, query, fresh_k, fresh_v, cache_k, cache_v, heads, ranks, tps, per_step, chunk
+    plen, owner, query, fresh_k, fresh_v, cache_k, cache_v, heads, ranks, tps, per_step, chunk
 ):
     parts = heads * ranks
     few, block = fresh_k.shape[0], cache_k.shape[0]
@@ -480,7 +533,7 @@
     return pl.pallas_call(
         functools.partial(fused_kernel, (heads, ranks, tps, per_step, chunk)),
         out_shape=jax.ShapeDtypeStruct((tps * few, heads * own_columns), b16),
-        in_specs=[pl.BlockSpec(memory_space=pltpu.VMEM)] * 3
+        in_specs=[pl.BlockSpec(memory_space=pltpu.SMEM)] * 2
         + [pl.BlockSpec(memory_space=pl.ANY)] * 5,
         out_specs=pl.BlockSpec(memory_space=pl.ANY),
         scratch_shapes=[
@@ -490,11 +543,14 @@
             pltpu.VMEM((steps, rows, width), b16),
             pltpu.VMEM((rows, own_columns), b16),
             pltpu.VMEM((2 * HEAD_SIZE, wide), b16),
-            pltpu.VMEM((chunk, wide), f32),
-            pltpu.VMEM((chunk, wide), f32),
-            pltpu.VMEM((1, wide), f32),
-            pltpu.VMEM((1, wide), f32),
-            pltpu.VMEM((HEAD_SIZE, wide), f32),
+            pltpu.VMEM((rows, rows), b16),
+            pltpu.VMEM((per_step, chunk, rows), f32),
+            pltpu.VMEM((per_step, chunk, rows), f32),
+            pltpu.VMEM((per_step, 1, rows), f32),
+            pltpu.VMEM((per_step, 1, rows), f32),
+            pltpu.VMEM((per_step, 1, rows), f32),
+            pltpu.VMEM((per_step, 1, rows), f32),
+            pltpu.VMEM((per_step, HEAD_SIZE, rows), f32),
             dma((2, heads, tps)),
             dma((2, heads, tps)),
             dma((2, heads)),
@@ -503,6 +559,7 @@
             dma((steps, heads * tps)),
             dma((steps, parts)),
             dma((steps, parts)),
+            dma((2 * parts,)),
         ]
         + rank_sems,
         compiler_params=pltpu.CompilerParams(
@@ -511,36 +568,26 @@
         cost_estimate=pl.CostEstimate(
             flops=4 * rows * own_columns * keys, bytes_accessed=100000000, transcendentals=0
         ),
-    )(plen, nat, pick, query, fresh_k, fresh_v, cache_k, cache_v)
+    )(plen, owner, query, fresh_k, fresh_v, cache_k, cache_v)
 
 
 def exchanged(
-    query, fresh_key_rows, fresh_value_rows, cached_key_rows, cached_value_rows, prefix_len, inverse
+    query,
+    fresh_key_rows,
+    fresh_value_rows,
+    cached_key_rows,
+    cached_value_rows,
+    prefix_len,
+    stripe_owner,
+    per_step,
+    chunk,
 ):
     parts, tps = lax.axis_size("cp"), lax.axis_size("tp")
     heads = cached_key_rows.shape[1] // HEAD_SIZE
     ranks = parts // heads
-    rank = lax.axis_index("cp") % ranks
-    few = fresh_key_rows.shape[0]
-    many = tps * few
-    stripe = many // parts
-    rows = heads * many
-    group = query.shape[1] // (tps * heads * HEAD_SIZE)
-    per_step = max(1, min(group, 512 // rows))
-    fresh = parts * many
-    chunk = min(512, fresh // 2)
-    z = jnp.arange(heads, dtype=jnp.int32)[None, :, None]
-    i = jnp.arange(stripe, dtype=jnp.int32)[None, None, :]
-    inside = inverse[:, None, None] * stripe + i
-    local = (z * many + inside).reshape(rows)
-    nat = ((z * ranks + rank) * many + inside).reshape(rows)
-    nat = jnp.tile(nat[None, :], (1, per_step))
-    pick = (local[:, None] == jnp.arange(rows, dtype=jnp.int32)[None, :]).astype(jnp.bfloat16)
-    plen = jnp.broadcast_to(prefix_len[None, :], nat.shape)
     landed = fused(
-        plen,
-        nat,
-        pick,
+        prefix_len,
+        stripe_owner,
         query,
         fresh_key_rows,
         fresh_value_rows,
@@ -552,11 +599,12 @@
         per_step,
         chunk,
     )
-    return (
-        landed.reshape(ranks, heads, stripe, landed.shape[1])
-        .transpose(1, 0, 2, 3)
-        .reshape(landed.shape)
-    )
+    rows = landed.shape[0]
+    stripe = rows // parts
+    order = jnp.arange(rows, dtype=jnp.int32).reshape(ranks, heads, stripe)
+    order = order.transpose(1, 0, 2).reshape(rows)
+    move = (order[:, None] == jnp.arange(rows, dtype=jnp.int32)[None, :]).astype(jnp.bfloat16)
+    return jnp.dot(move, landed, preferred_element_type=jnp.float32).astype(jnp.bfloat16)
 
 
 def plain(
@@ -640,21 +688,30 @@
     prefix_len,
     stripe_owner,
 ):
-    parts = lax.axis_size("cp")
+    parts, tps = lax.axis_size("cp"), lax.axis_size("tp")
     heads = cached_key_rows.shape[1] // HEAD_SIZE
     ranks = parts // heads
+    arrays = (query, fresh_key_rows, fresh_value_rows, cached_key_rows, cached_value_rows)
+    rows = heads * tps * fresh_key_rows.shape[0]
+    fresh = rows * ranks
+    slots = parts * cached_key_rows.shape[0]
+    group = query.shape[1] // (tps * heads * HEAD_SIZE)
+    per_step, chunk = math.gcd(4, group), 512
+    fits = (
+        heads > 1
+        and heads & (heads - 1) == 0
+        and ranks & (ranks - 1) == 0
+        and rows % (8 * parts) == 0
+        and rows % HEAD_SIZE == 0
+        and rows <= 512
+        and fresh % (2 * chunk) == 0
+        and slots % (8 * chunk) == 0
+    )
+    if fits:
+        return exchanged(*arrays, prefix_len, stripe_owner, per_step, chunk)
     order = jnp.arange(parts, dtype=jnp.int32)
     inverse = jnp.sum(jnp.where(stripe_owner[None, :] == order[:, None], order[None, :], 0), axis=1)
-    path = exchanged if heads > 1 and ranks & (ranks - 1) == 0 else plain
-    return path(
-        query,
-        fresh_key_rows,
-        fresh_value_rows,
-        cached_key_rows,
-        cached_value_rows,
-        prefix_len,
-        inverse,
-    )
+    return plain(*arrays, prefix_len, inverse)
 
 
 def solution(mesh):

time: 141 us -> 112 us (0.79)
  Pallas kernels: 134 us -> 109 us
  local copies, waits for them, and re-layouts: 4.99 us -> 0.09 us
  matrix products: 0 us -> 2.67 us
    pallas_call x1, Pallas kernels: 134 us -> 109 us  [fused(): pl.pallas_call(functools.partial(fused_kernel, (heads, ranks, tps, per_st...]
    dot_general x0 -> x1, matrix products: none -> 2.67 us  [exchanged(): jnp.dot(move, landed, preferred_element_type=jnp.float32)]
    reshape x2 -> x1, local copies, waits for them, and re-layouts: 2.56 us -> 0.09 us  [exchanged(): order = jnp.arange(rows, dtype=jnp.int32).reshape(ranks, heads, stripe)]
where the time goes in v2:
time: 112 us
  Pallas kernels  109 us (97%)
  matrix products  2.67 us (2%)
    pallas_call x1, Pallas kernels, fused(): pl.pallas_call(functools.partial(fused_kernel, (heads, ranks, tps, per_st...  109 us
    dot_general x1, matrix products, exchanged(): jnp.dot(move, landed, preferred_element_type=jnp.float32)  2.67 us

profile of v2, /device:TPU:0, one launch (start us, length us, event | category | flops | bytes accessed | tf_op | source)
XLA Modules:
  0.0 112.2 jit_solution(5455795852342631410)
XLA Ops:
  0.7 0.1 reshape.49
  0.8 108.8 %shard_map.73 = bf16[64,8192]{1,0:T(8,128)(2,1)} custom-call(s32[1]{0:T(128)S(6)} %copy.8.plen_ref, s32[16]{0:T(128)} %owner_ref.1, bf16[32,16384]{1,0:T(8,128)(2,1)} %query.1, bf16[32,1024]{1,0:T(8,128)(2,1)} %fresh_k.1, bf16[32,1024]{1,0:T(8,128)(2,1)} %fresh_v.1, bf16[512,512]{1,0:T(8,128)(2,1)} %cache_k.1, bf16[512,512]{1,0:T(8,128)(2,1)} %cache_v.1), custom_call_target="tpu_custom_call" | custom-call | flops 19327352832 | bytes 100000000 | tf_op jit(solution)/shard_map/pallas_call | solution.py:533
  109.5 2.7 %convolution_convert_fusion = bf16[64,8192]{1,0:T(8,128)(2,1)} fusion(bf16[64,8192]{1,0:T(8,128)(2,1)} %shard_map.73, s32[64]{0:T(128)S(1)} %reshape.49), kind=kOutput, calls=%fused_computation | convolution fusion | flops 67637248 | bytes 2097408 | tf_op jit(solution)/shard_map/dot_general | solution.py:607
  (1 shorter events, 0.0 us)

commit v3 on v2

--- a/solution.py
+++ b/solution.py
@@ -222,9 +222,8 @@
     def peer(s):
         other = row
         bit = 1
-        while bit <= s:
-            if s & bit:
-                other = other + bit - 2 * bit * ((other // bit) % 2)
+        while bit < heads:
+            other = other + (s // bit) % 2 * (bit - 2 * bit * ((other // bit) % 2))
             bit *= 2
         return other
 
@@ -258,17 +257,6 @@
 
     arrived = {}
     for s in shifts:
-        for a, source in enumerate((cache_k, cache_v)):
-            piece = cut(source, peer(s))
-            if s == 0:
-                copy = pltpu.make_async_copy(piece, place(a, me), z_recv.at[a, s])
-                copy.start()
-                arrived[a, s] = [copy.wait]
-            else:
-                copy = go(
-                    remote(piece, place(a, me), z_send.at[a, s], z_recv.at[a, s], at_column(s, 0))
-                )
-                arrived[a, s] = [copy.wait_recv]
         for a, source in enumerate((fresh_k, fresh_v)):
             waits = []
             for t in range(tps):
@@ -286,7 +274,19 @@
                         )
                     )
                     waits.append(copy.wait_recv)
-            arrived[2 + a, s] = waits
+            arrived[2 + a, s, 0] = waits
+    for s in shifts:
+        for a, source in enumerate((cache_k, cache_v)):
+            piece = cut(source, peer(s))
+            if s == 0:
+                copy = pltpu.make_async_copy(piece, place(a, me), z_recv.at[a, s])
+                copy.start()
+                arrived[a, s, 0] = [copy.wait]
+            else:
+                copy = go(
+                    remote(piece, place(a, me), z_send.at[a, s], z_recv.at[a, s], at_column(s, 0))
+                )
+                arrived[a, s, 0] = [copy.wait_recv]
 
     def query_copy(g, s, t, local):
         to = at_column(s, t)
@@ -306,35 +306,55 @@
 
     lax.fori_loop(0, steps, send_query, 0)
 
-    order = (2, 3, 0, 1)
-    held = [((a, s), a, s, rank) for s in shifts for a in order]
-    for level, partner in enumerate(partners):
-        send, receive = rank_sems[2 * level], rank_sems[2 * level + 1]
-        other = []
-        for number, (key, a, s, owner) in enumerate(held):
-            for wait in arrived.pop(key, ()):
-                wait()
-            index = peer(s) * ranks + owner
-            copy = go(
-                remote(
-                    place(a, index), place(a, index), send.at[number], receive.at[number], line[level]
+    relays, held = {}, {}
+    for s in shifts:
+        for a in range(4):
+            mine = [((a, s, 0), rank)]
+            for level, partner in enumerate(partners):
+                send, receive = rank_sems[2 * level], rank_sems[2 * level + 1]
+                bit = bits[level]
+                other = []
+                for k, (key, owner) in enumerate(mine):
+                    number = (s * 4 + a) * 2**level + k
+                    piece = place(a, peer(s) * ranks + owner)
+                    copy = remote(piece, piece, send.at[number], receive.at[number], line[level])
+                    started.append(copy)
+                    relays.setdefault((a // 2, s, level), []).append((key, copy))
+                    name = (a, s, level + 1, k)
+                    arrived[name] = [copy.wait_recv]
+                    other.append((name, owner + bit - 2 * bit * ((owner // bit) % 2)))
+                mine = mine + other
+            for key, owner in mine:
+                index = peer(s) * ranks + owner
+                held.setdefault((a // 2, s), []).append((key, a, index))
+    twin_copies = {}
+    for kind, s in held:
+        for key, a, index in held[kind, s]:
+            if a % 2 == 0:
+                size = tps * few if kind else block
+                start = index * size + (0 if kind else fresh)
+                twin_copies[key] = pltpu.make_async_copy(
+                    span(k2, start, size, size),
+                    k2.at[pl.ds(pl.multiple_of(start, size), size), pl.ds(HEAD_SIZE, HEAD_SIZE)],
+                    twin_sem.at[len(twin_copies)],
                 )
-            )
-            bit = bits[level]
-            name = (a, s, level + 1, number)
-            arrived[name] = [copy.wait_recv]
-            other.append((name, a, s, owner + bit - 2 * bit * ((owner // bit) % 2)))
-        held = held + other
-    twins = []
-
-    def twin(number, start, size):
-        copy = pltpu.make_async_copy(
-            span(k2, start, size, size),
-            k2.at[pl.ds(pl.multiple_of(start, size), size), pl.ds(HEAD_SIZE, HEAD_SIZE)],
-            twin_sem.at[number],
-        )
-        copy.start()
-        twins.append(copy)
+
+    def relay(kind, s, level):
+        for key, copy in relays[kind, s, level]:
+            if key[2] == level:
+                for wait in arrived[key]:
+                    wait()
+            copy.start()
+
+    levels = len(partners)
+    waves = sorted(((s, l) for s in shifts for l in range(levels)), key=lambda w: (sum(w), w[1]))
+    early = [w for w in waves if sum(w) < heads or heads <= 2]
+    late = [w for w in waves if w not in early]
+    for number, (s, level) in enumerate(early):
+        relay(0, s, level)
+        if s == 0:
+            for other in shifts:
+                relay(1, other, level)
 
     lane = lax.broadcasted_iota(jnp.int32, (rows, rows), 1)
     sorted_row = lax.broadcasted_iota(jnp.int32, (rows, rows), 0)
@@ -350,30 +370,37 @@
     z, inside = natural(sorted_row)
     pick_ref[...] = (z * (tps * few) + inside == lane).astype(jnp.float32).astype(jnp.bfloat16)
 
-    for key, a, s, owner in held:
-        for wait in arrived.pop(key, ()):
-            wait()
-        index = peer(s) * ranks + owner
-        if a == 0:
-            twin(len(twins), fresh + index * block, block)
-        elif a == 2:
-            twin(len(twins), index * (tps * few), tps * few)
-
     eye = (
         lax.broadcasted_iota(jnp.int32, (HEAD_SIZE, HEAD_SIZE), 0)
         == lax.broadcasted_iota(jnp.int32, (HEAD_SIZE, HEAD_SIZE), 1)
     ).astype(jnp.bfloat16)
 
-    def prepare(b, _):
-        at = pl.multiple_of(b * chunk, chunk)
-        vt[:, pl.ds(at, chunk)] = lax.dot_general(
-            eye, v_land[pl.ds(at, chunk), :], dn, preferred_element_type=jnp.float32
-        ).astype(jnp.bfloat16)
-        return 0
-
-    lax.fori_loop(0, keys // chunk, prepare, 0)
-    for copy in twins:
-        copy.wait()
+    def complete(kind, s, base, count):
+        items = held[kind, s]
+        for key, a, index in items:
+            if key[2] == levels:
+                for wait in arrived[key]:
+                    wait()
+            if key in twin_copies:
+                twin_copies[key].start()
+
+        def prepare(b, _):
+            at = pl.multiple_of(base + b * chunk, chunk)
+            vt[:, pl.ds(at, chunk)] = lax.dot_general(
+                eye, v_land[pl.ds(at, chunk), :], dn, preferred_element_type=jnp.float32
+            ).astype(jnp.bfloat16)
+            return 0
+
+        lax.fori_loop(0, count // chunk, prepare, 0)
+        for key, a, index in items:
+            if key in twin_copies:
+                twin_copies[key].wait()
+
+    for s in shifts:
+        complete(1, s, 0, fresh if s == heads - 1 else 0)
+    part = ranks * block
+    for s in range(2):
+        complete(0, s, fresh + peer(s) * part, part)
 
     slabs = ((s0, t0), (s1, t1))
 
@@ -425,9 +452,8 @@
 
     number = fresh // chunk
     units = slots // chunk
-    group = 4
+    group = part // chunk
     index = lax.broadcasted_iota(jnp.int32, (chunk, rows), 0)
-    sure = (units // 2 - 1) // group
 
     def step(g, _):
         for s, t in routes:
@@ -452,6 +478,9 @@
         def _():
             send_output(g - 1)
 
+        def base_of(s):
+            return pl.multiple_of(fresh + peer(s) * part, chunk)
+
         z, inside = natural(lax.broadcasted_iota(jnp.int32, (1, rows), 1))
         nat = (z * ranks + rank) * (tps * few) + inside
         for h in range(per_step):
@@ -461,36 +490,48 @@
                 if c + 1 < number:
                     score((c + 1) * chunk, (c + 1) % 2, h, index + (c + 1) * chunk <= nat)
                 else:
-                    score(fresh, 0, h, None)
+                    score(base_of(0), 0, h, index + peer(0) * part < plen_ref[0])
                 soften(c * chunk, c % 2, h, c == 0)
 
-        def batch(masked, j):
+        def batch(j, last):
+            here = peer(j) * part
+            beyond = None if last else peer(j + 1) * part
             for u in range(group):
-                slot = (j * group + u) * chunk
-                after = slot + chunk
-                mask = index + after < plen_ref[0] if masked else None
+                slot = here + u * chunk
+                after = slot + chunk if u + 1 < group else beyond
                 for h in range(per_step):
-                    score(pl.multiple_of(fresh + after, chunk), (u + 1) % 2, h, mask)
+                    if after is not None:
+                        score(
+                            pl.multiple_of(fresh + after, chunk),
+                            (u + 1) % 2,
+                            h,
+                            index + after < plen_ref[0],
+                        )
                     soften(pl.multiple_of(fresh + slot, chunk), u % 2, h, False)
+                    if after is None:
+                        finish_head(h)
             return 0
 
         def finish_head(h):
             columns = pl.ds(pl.multiple_of(g * width + h * HEAD_SIZE, HEAD_SIZE), HEAD_SIZE)
             o_buf[:, columns] = (acc_ref[h] / l_ref[h]).T.astype(o_buf.dtype)
 
-        if sure == 1:
-            batch(False, 0)
-        else:
-            lax.fori_loop(0, sure, lambda j, _: batch(False, j), 0)
-        lax.fori_loop(sure, units // group - 1, lambda j, _: batch(True, j), 0)
-        for u in range(units - group, units):
-            for h in range(per_step):
-                if u + 1 < units:
-                    after = (u + 1) * chunk
-                    score(fresh + after, (u + 1) % 2, h, index + after < plen_ref[0])
-                soften(fresh + u * chunk, u % 2, h, False)
-                if u + 1 == units:
-                    finish_head(h)
+        batch(0, False)
+
+        def middle(j, _):
+            for s in range(2, heads):
+
+                @pl.when((g == 0) & (j == s - 1))
+                def _():
+                    if s == 2:
+                        for w in late:
+                            relay(0, *w)
+                    complete(0, s, fresh + peer(s) * part, part)
+
+            return batch(j, False)
+
+        lax.fori_loop(1, heads - 1, middle, 0)
+        batch(heads - 1, True)
         return 0
 
     lax.fori_loop(0, steps, step, 0)
@@ -694,7 +735,6 @@
     arrays = (query, fresh_key_rows, fresh_value_rows, cached_key_rows, cached_value_rows)
     rows = heads * tps * fresh_key_rows.shape[0]
     fresh = rows * ranks
-    slots = parts * cached_key_rows.shape[0]
     group = query.shape[1] // (tps * heads * HEAD_SIZE)
     per_step, chunk = math.gcd(4, group), 512
     fits = (
@@ -705,7 +745,7 @@
         and rows % HEAD_SIZE == 0
         and rows <= 512
         and fresh % (2 * chunk) == 0
-        and slots % (8 * chunk) == 0
+        and ranks * cached_key_rows.shape[0] % (2 * chunk) == 0
     )
     if fits:
         return exchanged(*arrays, prefix_len, stripe_owner, per_step, chunk)

time: 112 us -> 109 us (0.973)
  Pallas kernels: 109 us -> 105 us
    pallas_call x1, Pallas kernels: 109 us -> 105 us  [fused(): pl.pallas_call(functools.partial(fused_kernel, (heads, ranks, tps, per_st...]
where the time goes in v3:
time: 109 us
  Pallas kernels  105 us (96%)
  matrix products  2.68 us (2%)
    pallas_call x1, Pallas kernels, fused(): pl.pallas_call(functools.partial(fused_kernel, (heads, ranks, tps, per_st...  105 us
    dot_general x1, matrix products, exchanged(): jnp.dot(move, landed, preferred_element_type=jnp.float32)  2.68 us

profile of v3, /device:TPU:0, one launch (start us, length us, event | category | flops | bytes accessed | tf_op | source)
XLA Modules:
  0.0 108.6 jit_solution(12797919586104260247)
XLA Ops:
  0.7 0.1 reshape.49
  0.8 105.2 %shard_map.73 = bf16[64,8192]{1,0:T(8,128)(2,1)} custom-call(s32[1]{0:T(128)S(6)} %copy.8.plen_ref, s32[16]{0:T(128)} %owner_ref.1, bf16[32,16384]{1,0:T(8,128)(2,1)} %query.1, bf16[32,1024]{1,0:T(8,128)(2,1)} %fresh_k.1, bf16[32,1024]{1,0:T(8,128)(2,1)} %fresh_v.1, bf16[512,512]{1,0:T(8,128)(2,1)} %cache_k.1, bf16[512,512]{1,0:T(8,128)(2,1)} %cache_v.1), custom_call_target="tpu_custom_call" | custom-call | flops 19327352832 | bytes 100000000 | tf_op jit(solution)/shard_map/pallas_call | solution.py:574
  106.0 2.7 %convolution_convert_fusion = bf16[64,8192]{1,0:T(8,128)(2,1)} fusion(bf16[64,8192]{1,0:T(8,128)(2,1)} %shard_map.73, s32[64]{0:T(128)S(1)} %reshape.49), kind=kOutput, calls=%fused_computation | convolution fusion | flops 67637248 | bytes 2097408 | tf_op jit(solution)/shard_map/dot_general | solution.py:648
  (1 shorter events, 0.0 us)

commit v4 on v3

--- a/solution.py
+++ b/solution.py
@@ -435,7 +435,7 @@
         m_ref[h] = m_new
 
     def output_copy(g, d):
-        to = (me + d) % parts
+        to = peer(d // ranks) * ranks + (rank + d % ranks) % ranks
         columns = pl.ds(pl.multiple_of(g * width, width), width)
         source = o_buf.at[pl.ds(pl.multiple_of(to * share, share), share), columns]
         target = out.at[

time: 109 us -> 110 us (level)
    pallas_call x1, Pallas kernels: 105 us -> 106 us  [fused(): pl.pallas_call(functools.partial(fused_kernel, (heads, ranks, tps, per_st...]
where the time goes in v4:
time: 110 us
  Pallas kernels  106 us (96%)
  matrix products  2.67 us (2%)
    pallas_call x1, Pallas kernels, fused(): pl.pallas_call(functools.partial(fused_kernel, (heads, ranks, tps, per_st...  106 us
    dot_general x1, matrix products, exchanged(): jnp.dot(move, landed, preferred_element_type=jnp.float32)  2.67 us

profile of v4, /device:TPU:0, one launch (start us, length us, event | category | flops | bytes accessed | tf_op | source)
XLA Modules:
  0.0 109.8 jit_solution(17733747276234096472)
XLA Ops:
  0.7 0.1 reshape.49
  0.8 106.3 %shard_map.73 = bf16[64,8192]{1,0:T(8,128)(2,1)} custom-call(s32[1]{0:T(128)S(6)} %copy.8.plen_ref, s32[16]{0:T(128)} %owner_ref.1, bf16[32,16384]{1,0:T(8,128)(2,1)} %query.1, bf16[32,1024]{1,0:T(8,128)(2,1)} %fresh_k.1, bf16[32,1024]{1,0:T(8,128)(2,1)} %fresh_v.1, bf16[512,512]{1,0:T(8,128)(2,1)} %cache_k.1, bf16[512,512]{1,0:T(8,128)(2,1)} %cache_v.1), custom_call_target="tpu_custom_call" | custom-call | flops 19327352832 | bytes 100000000 | tf_op jit(solution)/shard_map/pallas_call | solution.py:574
  107.1 2.7 %convolution_convert_fusion = bf16[64,8192]{1,0:T(8,128)(2,1)} fusion(bf16[64,8192]{1,0:T(8,128)(2,1)} %shard_map.73, s32[64]{0:T(128)S(1)} %reshape.49), kind=kOutput, calls=%fused_computation | convolution fusion | flops 67637248 | bytes 2097408 | tf_op jit(solution)/shard_map/dot_general | solution.py:648
  (1 shorter events, 0.0 us)
